TPU v7x, 32 devices: a whole 2x2x4 slice. The times are simulated.
32 devices in a mesh: cp: 8 (over z, x), tp: 4 (over y, core).
Axes of the slice: x: 2, y: 2, z: 4, core: 2. Of those that a mesh axis runs over, the one named last changes fastest.
Arguments:
- queries: bfloat16 [1536, 2048], P('cp', 'tp'), may hold values from -128 to 128
- keys: bfloat16 [1536, 256], P('cp'), may hold values from -6 to 6
- values: bfloat16 [1536, 256], P('cp'), may hold values from -6 to 6
- positions: int32 [1536], replicated, may hold values from 0 to 1535, as said below
- out_weight: bfloat16 [2048, 8192], P('tp'), may hold values from -0.125 to 0.125
Outputs:
- mixed: bfloat16 [1536, 8192], P(('cp', 'tp'))
Inputs may be any that keep to these rules, and one draw needn't show every extreme that they name: positions is a permutation of 0 to 1535. The tokens stored at indices d * 192 to (d + 1) * 192 - 1 form two runs of 96 consecutive positions, the first starting at b * 96 and the second at (15 - b) * 96 for some b, each b used by one d.
All inputs are finite; a program needn't handle non-finite values.
Results may differ from a plain program's by a relative error of at most 0.013.
Values may be sent and summed in bfloat16 or wider, within the bound.
A program may use at most 128 MiB of HBM per device.

v0:
```python
import jax
import jax.numpy as jnp
from jax import lax
from jax.sharding import PartitionSpec as P

HEAD = 128
GROUP = 8


def shards(queries, keys, values, positions, out_weight):
    tok_rows = queries.shape[0]
    head_count = queries.shape[1] // HEAD
    score_scale = HEAD ** (-0.5)
    kv_group = lax.axis_index("tp") * head_count // GROUP
    own_keys = lax.dynamic_slice_in_dim(keys, kv_group * HEAD, HEAD, 1)
    own_values = lax.dynamic_slice_in_dim(values, kv_group * HEAD, HEAD, 1)
    query_pos = lax.dynamic_slice_in_dim(positions, lax.axis_index("cp") * tok_rows, tok_rows, 0)
    local_queries = queries.reshape(tok_rows, head_count, HEAD)
    run_max = jnp.full((tok_rows, head_count), -1e30, jnp.float32)
    arrived_keys = lax.all_gather(own_keys, "cp", axis=0, tiled=True)
    arrived_values = lax.all_gather(own_values, "cp", axis=0, tiled=True)
    allowed = (positions[None, :] <= query_pos[:, None])[:, None, :]
    scores = (
        jnp.einsum("qhd,kd->qhk", local_queries, arrived_keys, preferred_element_type=jnp.float32)
        * score_scale
    )
    scores = jnp.where(allowed, scores, -1e30)
    new_max = jnp.maximum(run_max, jnp.max(scores, axis=-1))
    weights = jnp.where(allowed, jnp.exp(scores - new_max[:, :, None]), 0.0)
    run_sum = jnp.sum(weights, axis=-1)
    run_out = jnp.einsum(
        "qhk,kd->qhd",
        weights.astype(jnp.bfloat16),
        arrived_values,
        preferred_element_type=jnp.float32,
    )
    final_state = (new_max, run_sum, run_out)
    run_max, run_sum, run_out = final_state
    attended = (
        (run_out / run_sum[:, :, None]).astype(jnp.bfloat16).reshape(tok_rows, head_count * HEAD)
    )
    return lax.psum_scatter(
        jnp.dot(attended, out_weight, preferred_element_type=jnp.float32).astype(jnp.bfloat16),
        "tp",
        scatter_dimension=0,
        tiled=True,
    )


def solution(mesh):
    in_specs = (P("cp", "tp"), P("cp", None), P("cp", None), P(), P("tp", None))
    out_specs = P(("cp", "tp"), None)
    return jax.shard_map(shards, mesh=mesh, in_specs=in_specs, out_specs=out_specs, check_vma=False)
```

profile of v0, /device:TPU:0, one launch (start us, length us, event | category | flops | bytes accessed | tf_op | source)
XLA Modules:
  0.0 127.3 jit_solution(13655687156293303523)
XLA Ops:
  6.5 0.0 copy-start
  6.5 0.0 copy-start.1
  6.5 0.0 reduce-scatter.2.cloned.1.call-start
  6.5 0.8 constant_dynamic-slice_fusion.1
  7.4 32.8 %all_gather.6 = bf16[1536,128]{1,0:T(8,128)(2,1)S(1)} all-gather(bf16[192,128]{1,0:T(8,128)(2,1)S(1)} %constant_dynamic-slice_fusion.1), channel_id=1, replica_groups=mesh['cp'=8,'tp'=4] {'cp'}, dimensions={0}, use_global_device_ids=true | all-gather | bytes 442368 | tf_op jit(solution)/shard_map/all_gather | solution.py:20
  40.2 0.8 dynamic_slice.9
  40.9 0.9 broadcast_compare_fusion
  41.9 0.0 copy-done
  41.9 1.1 fusion
  43.0 0.0 copy-done.1
  43.0 31.0 %all_gather.7 = bf16[1536,128]{1,0:T(8,128)(2,1)S(1)} all-gather(bf16[192,128]{1,0:T(8,128)(2,1)S(1)} %constant_dynamic-slice_fusion), channel_id=1, replica_groups=mesh['cp'=8,'tp'=4] {'cp'}, dimensions={0}, use_global_device_ids=true | all-gather | bytes 442368 | tf_op jit(solution)/shard_map/all_gather | solution.py:21
  74.0 0.0 slice-start
  74.0 1.5 %fusion.1 = f32[192,4]{0,1:T(4,128)S(1)} fusion(f32[1536,192,4]{0,1,2:T(8,128)S(1)} %get-tuple-element.6, f32[192,4]{0,1:T(4,128)S(1)} %broadcast_maximum_fusion, pred[192,1536]{1,0:T(8,128)(4,1)S(1)} %broadcast_compare_fusion), kind=kLoop, calls=%fused_computation.4 | loop fusion | flops 5897472 | bytes 5019648 | tf_op jit(solution)/shard_map/reduce_sum | solution.py:30
  75.5 0.0 slice-start.1
  75.5 1.4 %fusion.12 = bf16[4,24,8,128]{3,2,1,0:T(8,128)(2,1)S(1)} fusion(f32[1536,192,4]{0,1,2:T(8,128)S(1)} %get-tuple-element.6, f32[192,4]{0,1:T(4,128)S(1)} %broadcast_maximum_fusion, pred[192,1536]{1,0:T(8,128)(4,1)S(1)} %broadcast_compare_fusion, bf16[1536,128]{1,0:T(8,128)(2,1)S(1)} %all_gather.7, f32[192,4]{0,1:T(4,128)S(1)} %fusion.1), kind=kOutput, calls=%fused_computation.10 | convolution fusion | flops 308084736 | bytes 5609472 | tf_op jit(solution)/shard_map/qhk,kd->qhd/dot_general | solution.py:31
  76.9 0.0 slice-done
  76.9 0.9 slice-done.1
  77.8 3.5 %convolution_convert_fusion = bf16[192,8192]{1,0:T(8,128)(2,1)} fusion(bf16[512,8192]{1,0:T(8,128)(2,1)S(1)} %bitcast.41, bf16[4,24,8,128]{3,2,1,0:T(8,128)(2,1)S(1)} %fusion.12), kind=kOutput, calls=%fused_computation | convolution fusion | flops 1612185600 | bytes 11730944 | tf_op jit(solution)/shard_map/dot_general | solution.py:43
  81.3 0.0 reduce-scatter.2.cloned.1.call-update
  81.3 39.2 %reduce-scatter.2.cloned.1.call-done = bf16[48,8192]{1,0:T(8,128)(2,1)} async-done(((bf16[192,8192]{1,0:T(8,128)(2,1)}), bf16[48,8192]{1,0:T(8,128)(2,1)}) %reduce-scatter.2.cloned.1.call-update) | async-done | bytes 786448 | tf_op jit(solution)/shard_map/reduce_scatter | solution.py:42
  (3 shorter events, 0.0 us)
Async XLA Ops:
  6.5 35.3 %copy-start = (bf16[192,512]{1,0:T(8,128)(2,1)S(1)}, bf16[192,512]{1,0:T(8,128)(2,1)}, u32[]{:S(2)}) copy-start(bf16[192,512]{1,0:T(8,128)(2,1)} %param.5) | copy-start | bytes 589828
  6.5 36.4 %copy-start.1 = (bf16[192,256]{1,0:T(8,128)(2,1)S(1)}, bf16[192,256]{1,0:T(8,128)(2,1)}, u32[]{:S(2)}) copy-start(bf16[192,256]{1,0:T(8,128)(2,1)} %param.7) | copy-start | bytes 294916
  6.5 114.0 %reduce-scatter.2.cloned.1.call-start = ((), (), s32[]{:S(2)}) async-start(), calls=%async_computation.1 | async-start | bytes 3932160 | tf_op jit(solution)/shard_map/reduce_scatter | solution.py:42
  74.0 2.9 %slice-start = ((s8[8388608]{0:T(1024)(128)(4,1)}), s8[4194304]{0:T(1024)(128)(4,1)S(1)}, s32[]{:S(2)}) async-start(s8[8388608]{0:T(1024)(128)(4,1)} %bitcast.40), calls=%async_computation.2 | async-start | bytes 8388608
  75.5 2.4 %slice-start.1 = ((s8[8388608]{0:T(1024)(128)(4,1)}), s8[4194304]{0:T(1024)(128)(4,1)S(1)}, s32[]{:S(2)}) async-start(s8[8388608]{0:T(1024)(128)(4,1)} %bitcast.40), calls=%async_computation.3 | async-start | bytes 8388608
Sparse Core Ops, SparseCore 0:
  81.4 39.0 reduce-scatter.1
where the time goes:
time: 128 us; the launch traced here: 127 us
  blocking collectives  63.7 us (50%)
  waiting for transfers between devices  39.2 us (31%)
  between operations  13.4 us (10%)
  matrix products  5.98 us (5%)
  local copies, waits for them, and re-layouts  2.58 us (2%)
  other arithmetic  2.41 us (2%)
    reduce_scatter x1, waiting for transfers between devices, shards(): lax.psum_scatter(jnp.dot(attended, out_weight, preferred_element_type=jnp...  39.2 us
    all_gather x1, blocking collectives, shards(): arrived_keys = lax.all_gather(own_keys, 'cp', axis=0, tiled=True)  32.8 us
    all_gather x1, blocking collectives, shards(): arrived_values = lax.all_gather(own_values, 'cp', axis=0, tiled=True)  31 us
    dot_general x1, matrix products, shards(): jnp.dot(attended, out_weight, preferred_element_type=jnp.float32)  3.47 us
  transfers between devices with their start and end apart: 1, of which 1 were waited for; matrix products, arithmetic and copies ran while one was open for 0% of the time, Pallas kernels for 0%

commit v1 on v0

v1 whole, which is shorter than its diff:
```python
import functools
import math

import jax
import jax.numpy as jnp
from jax import lax
from jax.experimental import pallas as pl
from jax.experimental.pallas import tpu as pltpu
from jax.sharding import PartitionSpec as P

HEAD = 128
GROUP = 8
CORES = 2
PAIR = 2
CHUNK = 512
W_PARTS = 4
LOG2E = math.log2(math.e)
NT = (((1,), (1,)), ((), ()))


def kernel(
    groups,
    pos,
    q,
    k,
    v,
    w,
    got,
    mine,
    qs,
    kv,
    wb,
    att,
    top,
    total,
    acc,
    far,
    near,
    load_sem,
    wl_sem,
    d_send,
    d_recv,
    x_send,
    x_recv,
    c_send,
    c_recv,
    w_send,
    w_recv,
    a_send,
    a_recv,
    y_send,
    y_recv,
    m_send,
    m_recv,
    m_local,
):
    tok = q.shape[0]
    heads = q.shape[1] // HEAD
    run = tok // 2
    part = run // CORES
    half_cols = w.shape[1] // CORES
    chunks = half_cols // CHUNK
    rows = heads * run
    span = PAIR * tok

    cp = lax.axis_index("cp")
    tp = lax.axis_index("tp")
    y = tp // CORES
    core = lax.rem(tp, CORES)
    mate = 1 - core
    far_y = 1 - y
    z = cp // PAIR
    side = lax.rem(cp, PAIR)
    kv_group = tp * heads // GROUP

    def dev(c, t):
        return {"cp": c, "tp": t}

    x_dev = dev(z * PAIR + 1 - side, tp)
    mate_dev = dev(cp, y * CORES + mate)

    def remote(src, dst, ssem, rsem, to):
        return pltpu.make_async_remote_copy(
            src_ref=src,
            dst_ref=dst,
            send_sem=ssem,
            recv_sem=rsem,
            device_id=to,
            device_id_type=pl.DeviceIdType.MESH,
        )

    def block(kind, zz, ss):
        return kv.at[kind, zz, pl.ds(pl.multiple_of(ss * tok, tok), tok)]

    cols = pl.ds(pl.multiple_of(kv_group * HEAD, HEAD), HEAD)
    loads = [
        pltpu.make_async_copy(k.at[:, cols], block(0, z, side), load_sem.at[0]),
        pltpu.make_async_copy(v.at[:, cols], block(1, z, side), load_sem.at[1]),
    ]
    q_loads = []
    for s, yy in ((0, far_y), (1, y)):
        for h in range(heads):
            q_loads.append(
                pltpu.make_async_copy(
                    q.at[pl.ds(pl.multiple_of(yy * run, run), run), pl.ds(h * HEAD, HEAD)],
                    qs.at[s, pl.ds(h * run, run)],
                    load_sem.at[2 + s * heads + h],
                )
            )
    piece = half_cols // W_PARTS
    w_loads, w_sends = [], []
    for i in range(W_PARTS):
        own = pl.ds(pl.multiple_of(core * half_cols + i * piece, piece), piece)
        other = pl.ds(pl.multiple_of(mate * half_cols + i * piece, piece), piece)
        here = pl.ds(i * piece, piece)
        w_loads.append(pltpu.make_async_copy(w.at[:, own], wb.at[0, :, here], wl_sem.at[i]))
        w_sends.append(
            remote(w.at[:, other], wb.at[1, :, here], w_send.at[i], w_recv.at[i], mate_dev)
        )
    for c in loads + q_loads:
        c.start()

    barrier = pltpu.get_barrier_semaphore()
    peers = [dev(lax.rem(z + off, groups) * PAIR + side, tp) for off in range(1, groups)]
    y_devs = [dev(cp, far_y * CORES + c) for c in range(CORES)]
    greet = peers + [x_dev, mate_dev] + y_devs
    for d in greet:
        pl.semaphore_signal(barrier, inc=1, device_id=d, device_id_type=pl.DeviceIdType.MESH)
    pl.semaphore_wait(barrier, len(greet))

    for c in loads:
        c.wait()
    own = block(core, z, side)
    sent = []
    x_own = remote(own, own, x_send.at[z], x_recv.at[z], x_dev)
    x_own.start()
    sent.append(x_own)
    for i, d in enumerate(peers):
        c = remote(own, own, d_send.at[i], d_recv.at[z], d)
        c.start()
        sent.append(c)
    for c in w_sends:
        c.start()
        sent.append(c)
    for c in w_loads:
        c.start()

    def hand(kind, zz, ss):
        b = block(kind, zz, ss)
        c = remote(b, b, c_send.at[zz, ss], c_recv.at[zz, ss], mate_dev)
        c.start()
        sent.append(c)

    def arrived_x(zz):
        b = block(core, zz, 1 - side)
        remote(b, b, x_send.at[zz], x_recv.at[zz], x_dev).wait_recv()
        hand(core, zz, 1 - side)

    def arrived_d(zz):
        b = block(core, zz, side)
        remote(b, b, d_send.at[0], d_recv.at[zz], x_dev).wait_recv()
        c = remote(b, b, x_send.at[zz], x_recv.at[zz], x_dev)
        c.start()
        sent.append(c)
        hand(core, zz, side)

    def arrived_c(zz, ss):
        b = block(mate, zz, ss)
        remote(b, b, c_send.at[zz, ss], c_recv.at[zz, ss], mate_dev).wait_recv()

    def attend(zz, s, first):
        yy = far_y if s == 0 else y
        keys = kv[0, zz]
        vals = kv[1, zz]
        scores = lax.dot_general(qs[s], keys, NT, preferred_element_type=jnp.float32)
        j = lax.broadcasted_iota(jnp.int32, (1, span), 1)
        base = zz * span
        key_pos = j + pos[base]
        for i in range(1, span // run):
            key_pos = jnp.where(j >= i * run, j + (pos[base + i * run] - i * run), key_pos)
        i = lax.rem(lax.broadcasted_iota(jnp.int32, (rows, 1), 0), run)
        query_pos = i + pos[cp * tok + yy * run]
        scores = jnp.where(key_pos <= query_pos, scores, -1e30)
        peak = jnp.max(scores, axis=1, keepdims=True)
        if not first:
            old = top[s]
            peak = jnp.maximum(old, peak)
        factor = HEAD**-0.5 * LOG2E
        weights = jnp.exp2((scores - peak) * factor)
        part_sum = jnp.sum(weights, axis=1, keepdims=True)
        part_out = jnp.dot(
            weights.astype(jnp.bfloat16), vals, preferred_element_type=jnp.float32
        )
        if not first:
            fade = jnp.exp2((old - peak) * factor)
            part_sum = total[s] * fade + part_sum
            part_out = acc[s] * fade + part_out
        top[s] = peak
        total[s] = part_sum
        acc[s] = part_out

    order = [lax.rem(z + groups - off, groups) for off in range(1, groups)]
    arrived_x(z)
    small = groups <= 4
    for c in q_loads:
        c.wait()

    def finish(s):
        out = (acc[s] / total[s]).astype(jnp.bfloat16)
        for h in range(heads):
            att[0, s, :, h * HEAD : (h + 1) * HEAD] = out[h * run : (h + 1) * run]
        c = remote(att.at[0, s], att.at[1, s], a_send.at[s], a_recv.at[s], mate_dev)
        c.start()
        sent.append(c)
        return c

    def own_group():
        arrived_c(z, 1 - side)
        attend(z, 0, True)
        attend(z, 1, True)

    if small:
        for zz in order[:-1]:
            arrived_d(zz)
        own_group()
        arrived_d(order[-1])
        for zz in order[:-1]:
            arrived_x(zz)
        for zz in order[:-2]:
            arrived_c(zz, side)
            arrived_c(zz, 1 - side)
            attend(zz, 0, False)
            attend(zz, 1, False)
        arrived_x(order[-1])
        for s in range(2):
            for zz in order[-2:]:
                if s == 0:
                    arrived_c(zz, side)
                    arrived_c(zz, 1 - side)
                attend(zz, s, False)
            if s == 0:
                swap_0 = finish(0)
        swap_1 = finish(1)
    else:
        for zz in order:
            arrived_d(zz)
        for zz in order:
            arrived_x(zz)
        own_group()

        def step(off, carry):
            zz = lax.rem(z + groups - off, groups)
            arrived_c(zz, side)
            arrived_c(zz, 1 - side)
            attend(zz, 0, False)
            attend(zz, 1, False)
            return carry

        lax.fori_loop(1, groups, step, 0)
        swap_0 = finish(0)
        swap_1 = finish(1)

    for c in w_loads:
        c.wait()
    for c in w_sends:
        c.wait_recv()

    def project(s, n):
        at = pl.ds(n * CHUNK, CHUNK)
        return (
            jnp.dot(att[0, s], wb[0, :, at], preferred_element_type=jnp.float32)
            + jnp.dot(att[1, s], wb[1, :, at], preferred_element_type=jnp.float32)
        ).astype(jnp.bfloat16)

    def place(ref, c, n):
        return ref.at[:, pl.ds(pl.multiple_of(c * half_cols + n * CHUNK, CHUNK), CHUNK)]

    swap_0.wait_recv()
    far_in = []
    for n in range(chunks):
        out = project(0, n)
        for c in range(CORES):
            far[n, c] = out[c * part : (c + 1) * part]
        for c in range(CORES):
            cc = remote(
                far.at[n, c], place(got, core, n), y_send.at[n, c], y_recv.at[n, core], y_devs[c]
            )
            cc.start()
            sent.append(cc)
            far_in.append((n, c))
    swap_1.wait_recv()
    local_copies, near_sends = [], []
    for n in range(chunks):
        out = project(1, n)
        for c in range(CORES):
            near[n, c] = out[c * part : (c + 1) * part]
        lc = pltpu.make_async_copy(near.at[n, core], place(mine, core, n), m_local.at[n])
        lc.start()
        local_copies.append(lc)
        rc = remote(near.at[n, mate], place(mine, core, n), m_send.at[n], m_recv.at[n], mate_dev)
        rc.start()
        near_sends.append(rc)

    for c in local_copies:
        c.wait()
    for n, c in enumerate(near_sends):
        c.wait_send()
        remote(
            near.at[n, mate], place(mine, mate, n), m_send.at[n], m_recv.at[n], mate_dev
        ).wait_recv()
    for c in sent:
        c.wait_send()
    for n, c in far_in:
        remote(
            far.at[n, c], place(got, c, n), y_send.at[n, c], y_recv.at[n, c], y_devs[c]
        ).wait_recv()


def shards(groups, queries, keys, values, positions, out_weight):
    tok, width = queries.shape
    heads = width // HEAD
    run = tok // 2
    part = run // CORES
    depth, cols = out_weight.shape
    half_cols = cols // CORES
    chunks = half_cols // CHUNK
    rows = heads * run
    dma = pltpu.SemaphoreType.DMA
    out = jax.ShapeDtypeStruct((part, cols), jnp.bfloat16)
    any_spec = pl.BlockSpec(memory_space=pl.ANY)
    got, mine = pl.pallas_call(
        functools.partial(kernel, groups),
        out_shape=(out, out),
        in_specs=[pl.BlockSpec(memory_space=pltpu.SMEM)] + [any_spec] * 4,
        out_specs=(any_spec, any_spec),
        scratch_shapes=[
            pltpu.VMEM((2, rows, HEAD), jnp.bfloat16),
            pltpu.VMEM((2, groups, PAIR * tok, HEAD), jnp.bfloat16),
            pltpu.VMEM((2, depth, half_cols), jnp.bfloat16),
            pltpu.VMEM((2, 2, run, width), jnp.bfloat16),
            pltpu.VMEM((2, rows, 1), jnp.float32),
            pltpu.VMEM((2, rows, 1), jnp.float32),
            pltpu.VMEM((2, rows, HEAD), jnp.float32),
            pltpu.VMEM((chunks, CORES, part, CHUNK), jnp.bfloat16),
            pltpu.VMEM((chunks, CORES, part, CHUNK), jnp.bfloat16),
            dma((2 + 2 * heads,)),
            dma((W_PARTS,)),
            dma((groups,)),
            dma((groups,)),
            dma((groups,)),
            dma((groups,)),
            dma((groups, PAIR)),
            dma((groups, PAIR)),
            dma((W_PARTS,)),
            dma((W_PARTS,)),
            dma((2,)),
            dma((2,)),
            dma((chunks, CORES)),
            dma((chunks, CORES)),
            dma((chunks,)),
            dma((chunks,)),
            dma((chunks,)),
        ],
        compiler_params=pltpu.CompilerParams(collective_id=0, has_side_effects=True),
    )(positions, queries, keys, values, out_weight)
    return (got.astype(jnp.float32) + mine.astype(jnp.float32)).astype(jnp.bfloat16)


def solution(mesh):
    groups = mesh.shape["cp"] // PAIR
    in_specs = (P("cp", "tp"), P("cp", None), P("cp", None), P(), P("tp", None))
    out_specs = P(("cp", "tp"), None)
    return jax.shard_map(
        functools.partial(shards, groups),
        mesh=mesh,
        in_specs=in_specs,
        out_specs=out_specs,
        check_vma=False,
    )
```

time: 128 us -> 43.6 us (0.34)
  blocking collectives: 63.7 us -> 0 us
  Pallas kernels: 0 us -> 40.9 us
  waiting for transfers between devices: 39.2 us -> 0 us
  between operations: 13.4 us -> 0.01 us
  matrix products: 5.98 us -> 0 us
  local copies, waits for them, and re-layouts: 2.58 us -> 0 us
    all_gather x2 -> x0, blocking collectives: 63.7 us -> none  [the longest x1 32.8 us: shards(): arrived_keys = lax.all_gather(own_keys, 'cp', axis=0, tiled=True)]
    pallas_call x0 -> x1, Pallas kernels: none -> 40.9 us  [shards(): pl.pallas_call(functools.partial(kernel, groups), out_shape=(out, out), i...]
    reduce_scatter x1 -> x0, waiting for transfers between devices: 39.2 us -> none  [shards(): lax.psum_scatter(jnp.dot(attended, out_weight, preferred_element_type=jnp...]
    dot_general x3 -> x0, matrix products: 5.98 us -> none  [the longest x1 3.47 us: shards(): jnp.dot(attended, out_weight, preferred_element_type=jnp.float32)]
    convert_element_type x0 -> x1, other arithmetic: none -> 2.43 us  [shards(): (got.astype(jnp.float32) + mine.astype(jnp.float32)).astype(jnp.bfloat16)]
    dynamic_slice x3 -> x0, local copies, waits for them, and re-layouts: 1.63 us -> none  [the longest x1 0.85 us: shards(): own_keys = lax.dynamic_slice_in_dim(keys, kv_group * HEAD, HEAD, 1)]
    reduce_sum x1 -> x0, other arithmetic: 1.48 us -> none  [shards(): run_sum = jnp.sum(weights, axis=-1)]
  transfers between devices with their start and end apart: 1 -> 0, of which waited for: 1 -> 0; matrix products, arithmetic and copies ran while one was open for 0% -> 0% of each run, Pallas kernels for 0% -> 0%
where the time goes in v1:
time: 43.6 us; the launch traced here: 43.3 us
  Pallas kernels  40.9 us (94%)
  other arithmetic  2.43 us (6%)
    pallas_call x1, Pallas kernels, shards(): pl.pallas_call(functools.partial(kernel, groups), out_shape=(out, out), i...  40.9 us
    convert_element_type x1, other arithmetic, shards(): (got.astype(jnp.float32) + mine.astype(jnp.float32)).astype(jnp.bfloat16)  2.43 us

profile of v1, /device:TPU:0, one launch (start us, length us, event | category | flops | bytes accessed | tf_op | source)
XLA Modules:
  0.0 43.3 jit_solution(13762193051656287587)
XLA Ops:
  0.0 40.9 %shard_map.55 = (bf16[48,8192]{1,0:T(8,128)(2,1)}, bf16[48,8192]{1,0:T(8,128)(2,1)}) custom-call(s32[1536]{0:T(1024)} %pos.1, bf16[192,512]{1,0:T(8,128)(2,1)} %q.1, bf16[192,256]{1,0:T(8,128)(2,1)} %k.1, bf16[192,256]{1,0:T(8,128)(2,1)} %v.1, bf16[512,8192]{1,0:T(8,128)(2,1)} %w.1), custom_call_target="tpu_custom_call" | custom-call | tf_op jit(solution)/shard_map/pallas_call | solution.py:331
  40.9 2.4 %add_convert_fusion = bf16[48,8192]{1,0:T(8,128)(2,1)} fusion(bf16[48,8192]{1,0:T(8,128)(2,1)} %get-tuple-element.8, bf16[48,8192]{1,0:T(8,128)(2,1)} %get-tuple-element.7), kind=kLoop, calls=%fused_computation | loop fusion | flops 1572864 | bytes 2359296 | tf_op jit(solution)/shard_map/convert_element_type | solution.py:366

commit v2 on v1

--- a/solution.py
+++ b/solution.py
@@ -13,7 +13,8 @@
 CORES = 2
 PAIR = 2
 CHUNK = 512
-W_PARTS = 4
+W_PARTS = 8
+PIECES = 2
 LOG2E = math.log2(math.e)
 NT = (((1,), (1,)), ((), ()))
 
@@ -39,6 +40,7 @@
     load_sem,
     wl_sem,
     d_send,
+    o_send,
     d_recv,
     x_send,
     x_recv,
@@ -89,8 +91,11 @@
             device_id_type=pl.DeviceIdType.MESH,
         )
 
-    def block(kind, zz, ss):
-        return kv.at[kind, zz, pl.ds(pl.multiple_of(ss * tok, tok), tok)]
+    def block(kind, zz, ss, at=None):
+        if at is None:
+            return kv.at[kind, zz, pl.ds(pl.multiple_of(ss * tok, tok), tok)]
+        size = tok // PIECES
+        return kv.at[kind, zz, pl.ds(pl.multiple_of(ss * tok + at * size, size), size)]
 
     cols = pl.ds(pl.multiple_of(kv_group * HEAD, HEAD), HEAD)
     loads = [
@@ -121,52 +126,84 @@
         c.start()
 
     barrier = pltpu.get_barrier_semaphore()
-    peers = [dev(lax.rem(z + off, groups) * PAIR + side, tp) for off in range(1, groups)]
     y_devs = [dev(cp, far_y * CORES + c) for c in range(CORES)]
-    greet = peers + [x_dev, mate_dev] + y_devs
-    for d in greet:
+    has_left = z > 0
+    has_right = z < groups - 1
+    left = dev(jnp.maximum(z - 1, 0) * PAIR + side, tp)
+    right = dev(jnp.minimum(z + 1, groups - 1) * PAIR + side, tp)
+
+    def greet(d):
         pl.semaphore_signal(barrier, inc=1, device_id=d, device_id_type=pl.DeviceIdType.MESH)
-    pl.semaphore_wait(barrier, len(greet))
+
+    always = [x_dev, mate_dev] + y_devs
+    for d in always:
+        greet(d)
+    pl.when(has_left)(lambda: greet(left))
+    pl.when(has_right)(lambda: greet(right))
+    sides = jnp.where(has_left, 1, 0) + jnp.where(has_right, 1, 0)
+    pl.semaphore_wait(barrier, len(always) + sides)
 
     for c in loads:
         c.wait()
-    own = block(core, z, side)
     sent = []
-    x_own = remote(own, own, x_send.at[z], x_recv.at[z], x_dev)
-    x_own.start()
-    sent.append(x_own)
-    for i, d in enumerate(peers):
-        c = remote(own, own, d_send.at[i], d_recv.at[z], d)
-        c.start()
-        sent.append(c)
-    for c in w_sends:
-        c.start()
-        sent.append(c)
+    sent_if = []
+
+    def start(c, when=None):
+        if when is None:
+            c.start()
+            sent.append(c)
+        else:
+            pl.when(when)(c.start)
+            sent_if.append((when, c))
+
+    for p in range(PIECES):
+        own = block(core, z, side, p)
+        start(remote(own, own, d_send.at[z, p], d_recv.at[z, p], left), has_left)
+        start(remote(own, own, o_send.at[p], d_recv.at[z, p], right), has_right)
+        start(remote(own, own, x_send.at[z, p], x_recv.at[z, p], x_dev))
+    waiting = list(w_sends)
+
+    def swap_w(count):
+        for c in waiting[:count]:
+            start(c)
+        del waiting[:count]
+
+    swap_w(3)
     for c in w_loads:
         c.start()
 
-    def hand(kind, zz, ss):
-        b = block(kind, zz, ss)
-        c = remote(b, b, c_send.at[zz, ss], c_recv.at[zz, ss], mate_dev)
-        c.start()
-        sent.append(c)
+    near_z = jnp.minimum(z, groups - 1 - z)
+    long_side = jnp.where(2 * z < groups, 1, -1)
+
+    def arrival(i):
+        turn = jnp.where(lax.rem(i, 2) == 1, -((i + 1) // 2), i // 2)
+        return z + jnp.where(i <= 2 * near_z, turn, long_side * (i - near_z))
+
+    def hand(zz, ss, p):
+        b = block(core, zz, ss, p)
+        start(remote(b, b, c_send.at[zz, ss, p], c_recv.at[zz, ss, p], mate_dev))
 
     def arrived_x(zz):
-        b = block(core, zz, 1 - side)
-        remote(b, b, x_send.at[zz], x_recv.at[zz], x_dev).wait_recv()
-        hand(core, zz, 1 - side)
+        for p in range(PIECES):
+            b = block(core, zz, 1 - side, p)
+            remote(b, b, x_send.at[zz, p], x_recv.at[zz, p], x_dev).wait_recv()
+            hand(zz, 1 - side, p)
 
     def arrived_d(zz):
-        b = block(core, zz, side)
-        remote(b, b, d_send.at[0], d_recv.at[zz], x_dev).wait_recv()
-        c = remote(b, b, x_send.at[zz], x_recv.at[zz], x_dev)
-        c.start()
-        sent.append(c)
-        hand(core, zz, side)
+        onward = jnp.where(zz < z, z + 1, z - 1)
+        inside = (onward >= 0) & (onward < groups)
+        to = dev(jnp.clip(onward, 0, groups - 1) * PAIR + side, tp)
+        for p in range(PIECES):
+            b = block(core, zz, side, p)
+            remote(b, b, d_send.at[zz, p], d_recv.at[zz, p], x_dev).wait_recv()
+            start(remote(b, b, d_send.at[zz, p], d_recv.at[zz, p], to), inside)
+            start(remote(b, b, x_send.at[zz, p], x_recv.at[zz, p], x_dev))
+            hand(zz, side, p)
 
     def arrived_c(zz, ss):
-        b = block(mate, zz, ss)
-        remote(b, b, c_send.at[zz, ss], c_recv.at[zz, ss], mate_dev).wait_recv()
+        for p in range(PIECES):
+            b = block(mate, zz, ss, p)
+            remote(b, b, c_send.at[zz, ss, p], c_recv.at[zz, ss, p], mate_dev).wait_recv()
 
     def attend(zz, s, first):
         yy = far_y if s == 0 else y
@@ -199,11 +236,8 @@
         total[s] = part_sum
         acc[s] = part_out
 
-    order = [lax.rem(z + groups - off, groups) for off in range(1, groups)]
     arrived_x(z)
-    small = groups <= 4
-    for c in q_loads:
-        c.wait()
+    swap_w(1)
 
     def finish(s):
         out = (acc[s] / total[s]).astype(jnp.bfloat16)
@@ -214,44 +248,55 @@
         sent.append(c)
         return c
 
-    def own_group():
+    def arrived_group(zz):
+        arrived_c(zz, side)
+        arrived_c(zz, 1 - side)
+
+    def load_q():
+        for c in q_loads:
+            c.wait()
+
+    if groups == 4:
+        z1, z2, z3 = (arrival(i) for i in range(1, groups))
+        arrived_d(z1)
+        swap_w(1)
         arrived_c(z, 1 - side)
+        load_q()
+        attend(z, 0, True)
+        arrived_d(z2)
+        swap_w(1)
+        attend(z, 1, True)
+        arrived_x(z1)
+        arrived_d(z3)
+        swap_w(1)
+        arrived_group(z1)
+        attend(z1, 0, False)
+        attend(z1, 1, False)
+        arrived_x(z2)
+        arrived_group(z2)
+        attend(z2, 0, False)
+        attend(z2, 1, False)
+        arrived_x(z3)
+        swap_w(W_PARTS)
+        arrived_group(z3)
+        attend(z3, 0, False)
+        swap_0 = finish(0)
+        attend(z3, 1, False)
+        swap_1 = finish(1)
+    else:
+        for i in range(1, groups):
+            arrived_d(arrival(i))
+        for i in range(1, groups):
+            arrived_x(arrival(i))
+        swap_w(W_PARTS)
+        arrived_c(z, 1 - side)
+        load_q()
         attend(z, 0, True)
         attend(z, 1, True)
 
-    if small:
-        for zz in order[:-1]:
-            arrived_d(zz)
-        own_group()
-        arrived_d(order[-1])
-        for zz in order[:-1]:
-            arrived_x(zz)
-        for zz in order[:-2]:
-            arrived_c(zz, side)
-            arrived_c(zz, 1 - side)
-            attend(zz, 0, False)
-            attend(zz, 1, False)
-        arrived_x(order[-1])
-        for s in range(2):
-            for zz in order[-2:]:
-                if s == 0:
-                    arrived_c(zz, side)
-                    arrived_c(zz, 1 - side)
-                attend(zz, s, False)
-            if s == 0:
-                swap_0 = finish(0)
-        swap_1 = finish(1)
-    else:
-        for zz in order:
-            arrived_d(zz)
-        for zz in order:
-            arrived_x(zz)
-        own_group()
-
-        def step(off, carry):
-            zz = lax.rem(z + groups - off, groups)
-            arrived_c(zz, side)
-            arrived_c(zz, 1 - side)
+        def step(i, carry):
+            zz = arrival(i)
+            arrived_group(zz)
             attend(zz, 0, False)
             attend(zz, 1, False)
             return carry
@@ -310,6 +355,8 @@
         ).wait_recv()
     for c in sent:
         c.wait_send()
+    for when, c in sent_if:
+        pl.when(when)(c.wait_send)
     for n, c in far_in:
         remote(
             far.at[n, c], place(got, c, n), y_send.at[n, c], y_recv.at[n, c], y_devs[c]
@@ -326,13 +373,13 @@
     chunks = half_cols // CHUNK
     rows = heads * run
     dma = pltpu.SemaphoreType.DMA
-    out = jax.ShapeDtypeStruct((part, cols), jnp.bfloat16)
+    out = pltpu.VMEM((part, cols), jnp.bfloat16)
     any_spec = pl.BlockSpec(memory_space=pl.ANY)
     got, mine = pl.pallas_call(
         functools.partial(kernel, groups),
         out_shape=(out, out),
         in_specs=[pl.BlockSpec(memory_space=pltpu.SMEM)] + [any_spec] * 4,
-        out_specs=(any_spec, any_spec),
+        out_specs=(pl.BlockSpec(memory_space=pltpu.VMEM),) * 2,
         scratch_shapes=[
             pltpu.VMEM((2, rows, HEAD), jnp.bfloat16),
             pltpu.VMEM((2, groups, PAIR * tok, HEAD), jnp.bfloat16),
@@ -345,12 +392,13 @@
             pltpu.VMEM((chunks, CORES, part, CHUNK), jnp.bfloat16),
             dma((2 + 2 * heads,)),
             dma((W_PARTS,)),
-            dma((groups,)),
-            dma((groups,)),
-            dma((groups,)),
-            dma((groups,)),
-            dma((groups, PAIR)),
-            dma((groups, PAIR)),
+            dma((groups, PIECES)),
+            dma((PIECES,)),
+            dma((groups, PIECES)),
+            dma((groups, PIECES)),
+            dma((groups, PIECES)),
+            dma((groups, PAIR, PIECES)),
+            dma((groups, PAIR, PIECES)),
             dma((W_PARTS,)),
             dma((W_PARTS,)),
             dma((2,)),

time: 43.6 us -> 44.1 us (1.011)
  Pallas kernels: 40.9 us -> 42.8 us
  other arithmetic: 2.43 us -> 1.06 us
    pallas_call x1, Pallas kernels: 40.9 us -> 42.8 us  [shards(): pl.pallas_call(functools.partial(kernel, groups), out_shape=(out, out), i...]
    convert_element_type x1, other arithmetic: 2.43 us -> 1.06 us  [shards(): (got.astype(jnp.float32) + mine.astype(jnp.float32)).astype(jnp.bfloat16)]
where the time goes in v2:
time: 44.1 us; the launch traced here: 43.9 us
  Pallas kernels  42.8 us (97%)
  other arithmetic  1.06 us (2%)
    pallas_call x1, Pallas kernels, shards(): pl.pallas_call(functools.partial(kernel, groups), out_shape=(out, out), i...  42.8 us
    convert_element_type x1, other arithmetic, shards(): (got.astype(jnp.float32) + mine.astype(jnp.float32)).astype(jnp.bfloat16)  1.06 us

profile of v2, /device:TPU:0, one launch (start us, length us, event | category | flops | bytes accessed | tf_op | source)
XLA Modules:
  0.0 43.9 jit_solution(14367913309004621482)
XLA Ops:
  0.0 42.8 %shard_map.55 = (bf16[48,8192]{1,0:T(8,128)(2,1)S(1)}, bf16[48,8192]{1,0:T(8,128)(2,1)S(1)}) custom-call(s32[1536]{0:T(1024)} %pos.1, bf16[192,512]{1,0:T(8,128)(2,1)} %q.1, bf16[192,256]{1,0:T(8,128)(2,1)} %k.1, bf16[192,256]{1,0:T(8,128)(2,1)} %v.1, bf16[512,8192]{1,0:T(8,128)(2,1)} %w.1), custom_call_target="tpu_custom_call" | custom-call | tf_op jit(solution)/shard_map/pallas_call | solution.py:378
  42.8 1.1 %add_convert_fusion = bf16[48,8192]{1,0:T(8,128)(2,1)} fusion(bf16[48,8192]{1,0:T(8,128)(2,1)S(1)} %get-tuple-element.8, bf16[48,8192]{1,0:T(8,128)(2,1)S(1)} %get-tuple-element.7), kind=kLoop, calls=%fused_computation | loop fusion | flops 1572864 | bytes 2359296 | tf_op jit(solution)/shard_map/convert_element_type | solution.py:414

commit v3 on v1

--- a/solution.py
+++ b/solution.py
@@ -13,20 +13,22 @@
 CORES = 2
 PAIR = 2
 CHUNK = 512
-W_PARTS = 4
+W_PARTS = 8
 LOG2E = math.log2(math.e)
 NT = (((1,), (1,)), ((), ()))
 
 
 def kernel(
     groups,
-    pos,
+    pos_in,
     q,
     k,
     v,
     w,
     got,
     mine,
+    pos,
+    pos_sem,
     qs,
     kv,
     wb,
@@ -117,11 +119,12 @@
         w_sends.append(
             remote(w.at[:, other], wb.at[1, :, here], w_send.at[i], w_recv.at[i], mate_dev)
         )
-    for c in loads + q_loads:
+    pos_load = pltpu.make_async_copy(pos_in, pos, pos_sem)
+    for c in loads + q_loads + [pos_load]:
         c.start()
 
     barrier = pltpu.get_barrier_semaphore()
-    peers = [dev(lax.rem(z + off, groups) * PAIR + side, tp) for off in range(1, groups)]
+    peers = [dev(lax.rem(z + off, groups) * PAIR + side, tp) for off in range(groups - 1, 0, -1)]
     y_devs = [dev(cp, far_y * CORES + c) for c in range(CORES)]
     greet = peers + [x_dev, mate_dev] + y_devs
     for d in greet:
@@ -139,9 +142,15 @@
         c = remote(own, own, d_send.at[i], d_recv.at[z], d)
         c.start()
         sent.append(c)
-    for c in w_sends:
-        c.start()
-        sent.append(c)
+    waiting = list(w_sends)
+
+    def swap_w(count):
+        for c in waiting[:count]:
+            c.start()
+            sent.append(c)
+        del waiting[:count]
+
+    swap_w(3)
     for c in w_loads:
         c.start()
 
@@ -199,10 +208,10 @@
         total[s] = part_sum
         acc[s] = part_out
 
-    order = [lax.rem(z + groups - off, groups) for off in range(1, groups)]
+    order = [lax.rem(z + groups - off, groups) for off in range(groups - 1, 0, -1)]
     arrived_x(z)
     small = groups <= 4
-    for c in q_loads:
+    for c in q_loads + [pos_load]:
         c.wait()
 
     def finish(s):
@@ -220,32 +229,40 @@
         attend(z, 1, True)
 
     if small:
-        for zz in order[:-1]:
-            arrived_d(zz)
-        own_group()
-        arrived_d(order[-1])
-        for zz in order[:-1]:
-            arrived_x(zz)
-        for zz in order[:-2]:
-            arrived_c(zz, side)
-            arrived_c(zz, 1 - side)
-            attend(zz, 0, False)
-            attend(zz, 1, False)
-        arrived_x(order[-1])
-        for s in range(2):
-            for zz in order[-2:]:
-                if s == 0:
-                    arrived_c(zz, side)
-                    arrived_c(zz, 1 - side)
-                attend(zz, s, False)
-            if s == 0:
-                swap_0 = finish(0)
+        z1, z2, z3 = order
+        arrived_d(z1)
+        swap_w(1)
+        arrived_c(z, 1 - side)
+        attend(z, 0, True)
+        arrived_d(z2)
+        swap_w(1)
+        attend(z, 1, True)
+        arrived_d(z3)
+        arrived_x(z1)
+        swap_w(1)
+        arrived_c(z1, side)
+        arrived_c(z1, 1 - side)
+        attend(z1, 0, False)
+        arrived_x(z2)
+        attend(z1, 1, False)
+        arrived_x(z3)
+        swap_w(W_PARTS)
+        arrived_c(z2, side)
+        arrived_c(z2, 1 - side)
+        attend(z2, 0, False)
+        arrived_c(z3, side)
+        arrived_c(z3, 1 - side)
+        attend(z3, 0, False)
+        swap_0 = finish(0)
+        attend(z2, 1, False)
+        attend(z3, 1, False)
         swap_1 = finish(1)
     else:
         for zz in order:
             arrived_d(zz)
         for zz in order:
             arrived_x(zz)
+        swap_w(W_PARTS)
         own_group()
 
         def step(off, carry):
@@ -326,14 +343,16 @@
     chunks = half_cols // CHUNK
     rows = heads * run
     dma = pltpu.SemaphoreType.DMA
-    out = jax.ShapeDtypeStruct((part, cols), jnp.bfloat16)
+    out = pltpu.VMEM((part, cols), jnp.bfloat16)
     any_spec = pl.BlockSpec(memory_space=pl.ANY)
     got, mine = pl.pallas_call(
         functools.partial(kernel, groups),
         out_shape=(out, out),
-        in_specs=[pl.BlockSpec(memory_space=pltpu.SMEM)] + [any_spec] * 4,
-        out_specs=(any_spec, any_spec),
+        in_specs=[any_spec] * 5,
+        out_specs=(pl.BlockSpec(memory_space=pltpu.VMEM),) * 2,
         scratch_shapes=[
+            pltpu.SMEM(positions.shape, jnp.int32),
+            dma(()),
             pltpu.VMEM((2, rows, HEAD), jnp.bfloat16),
             pltpu.VMEM((2, groups, PAIR * tok, HEAD), jnp.bfloat16),
             pltpu.VMEM((2, depth, half_cols), jnp.bfloat16),

time: 43.6 us -> 39.8 us (0.913)
  Pallas kernels: 40.9 us -> 38.5 us
  other arithmetic: 2.43 us -> 1.06 us
    pallas_call x1, Pallas kernels: 40.9 us -> 38.5 us  [shards(): pl.pallas_call(functools.partial(kernel, groups), out_shape=(out, out), i...]
    convert_element_type x1, other arithmetic: 2.43 us -> 1.06 us  [shards(): (got.astype(jnp.float32) + mine.astype(jnp.float32)).astype(jnp.bfloat16)]
where the time goes in v3:
time: 39.8 us; the launch traced here: 39.6 us
  Pallas kernels  38.5 us (97%)
  other arithmetic  1.06 us (3%)
    pallas_call x1, Pallas kernels, shards(): pl.pallas_call(functools.partial(kernel, groups), out_shape=(out, out), i...  38.5 us
    convert_element_type x1, other arithmetic, shards(): (got.astype(jnp.float32) + mine.astype(jnp.float32)).astype(jnp.bfloat16)  1.06 us

profile of v3, /device:TPU:0, one launch (start us, length us, event | category | flops | bytes accessed | tf_op | source)
XLA Modules:
  0.0 39.6 jit_solution(12252869447843659588)
XLA Ops:
  0.0 38.5 %shard_map.55 = (bf16[48,8192]{1,0:T(8,128)(2,1)S(1)}, bf16[48,8192]{1,0:T(8,128)(2,1)S(1)}) custom-call(s32[1536]{0:T(1024)} %pos_in.1, bf16[192,512]{1,0:T(8,128)(2,1)} %q.1, bf16[192,256]{1,0:T(8,128)(2,1)} %k.1, bf16[192,256]{1,0:T(8,128)(2,1)} %v.1, bf16[512,8192]{1,0:T(8,128)(2,1)} %w.1), custom_call_target="tpu_custom_call" | custom-call | tf_op jit(solution)/shard_map/pallas_call | solution.py:348
  38.5 1.1 %add_convert_fusion = bf16[48,8192]{1,0:T(8,128)(2,1)} fusion(bf16[48,8192]{1,0:T(8,128)(2,1)S(1)} %get-tuple-element.8, bf16[48,8192]{1,0:T(8,128)(2,1)S(1)} %get-tuple-element.7), kind=kLoop, calls=%fused_computation | loop fusion | flops 1572864 | bytes 2359296 | tf_op jit(solution)/shard_map/convert_element_type | solution.py:385
